TPU v7x, 32 devices: a whole 2x2x4 slice. The times are simulated.
32 devices in a mesh: dp: 8 (over z, x), shard: 4 (over y, core).
Axes of the slice: x: 2, y: 2, z: 4, core: 2. Of those that a mesh axis runs over, the one named last changes fastest.
Arguments:
- tokens: bfloat16 [128, 3584], P('dp', 'shard'), may hold values from -6 to 6
- targets: bfloat16 [128, 3584], P('dp', 'shard'), may hold values from -6 to 6
- task_of_token: int32 [128], P('dp'), may hold values from 0 to 15, never falling along the last dimension, each value on 1 to 16 neighbouring positions
- up_weight: bfloat16 [18944, 3584], P('dp', 'shard'), may hold values from -0.09375 to 0.09375
- down_weight: bfloat16 [18944, 3584], P('dp', 'shard'), may hold values from -0.046875 to 0.046875
- outer_up: bfloat16 [18944, 3584], P('dp', 'shard'), may hold values from -6 to 6
- outer_down: bfloat16 [18944, 3584], P('dp', 'shard'), may hold values from -6 to 6
Outputs:
- meta_up: float32 [18944, 3584], P('dp', 'shard')
- meta_down: float32 [18944, 3584], P('dp', 'shard')
Inputs may be any that keep to these rules, and one draw needn't show every extreme that they name: `task_of_token`: task numbers never fall along the tokens; every task has 1 to 16 tokens, and some task has exactly 16.
All inputs are finite; a program needn't handle non-finite values.
Results may differ from a plain program's by a relative error of at most 0.001.
Values may be sent and summed in bfloat16 or wider, within the bound.
A program may use at most 64 MiB of HBM per device.

v0:
```python
import jax
import jax.numpy as jnp
from jax import lax
from jax.sharding import PartitionSpec as P

TASKS = 16
ITERS = 2


def sigmoid_parts(linear_part):
    argument = linear_part.astype(jnp.float32)
    logistic = jax.nn.sigmoid(argument)
    derivative = logistic * (1.0 + argument * (1.0 - logistic))
    second_order = logistic * (1.0 - logistic) * (2.0 + argument * (1.0 - 2.0 * logistic))
    return (argument * logistic, derivative, second_order)


def contract_last(left_side, right_side):
    return lax.dot_general(
        left_side, right_side, (((1,), (1,)), ((), ())), preferred_element_type=jnp.float32
    )


def contract_first(left_side, right_side):
    return lax.dot_general(
        left_side, right_side, (((0,), (0,)), ((), ())), preferred_element_type=jnp.float32
    )


def over_hidden(partial_value):
    portion = lax.psum_scatter(
        partial_value.astype(jnp.bfloat16), "shard", scatter_dimension=1, tiled=True
    )
    return lax.all_gather(portion, "shard", axis=1, tiled=True)


def over_tokens(term_fn, row_count):
    return lax.psum_scatter(
        term_fn(jnp.int32(0), row_count * lax.axis_size("dp")).astype(jnp.bfloat16),
        "dp",
        scatter_dimension=0,
        tiled=True,
    ).astype(jnp.float32)


def all_tokens(local_part):
    return lax.all_gather(local_part, "dp", axis=0, tiled=True)


def paired_sum(first_up, second_up, first_down, second_down):
    return jnp.sum(first_up * second_up) + jnp.sum(first_down * second_down)


def both_totals(residual_up, residual_down, image_up, image_down):
    return lax.psum(
        (
            paired_sum(residual_up, residual_up, residual_down, residual_down),
            paired_sum(residual_up, image_up, residual_down, image_down),
        ),
        ("dp", "shard"),
    )


def body(tokens, targets, task_of_token, up_weight, down_weight, outer_up, outer_down):
    row_count = tokens.shape[0]
    task_index = jnp.arange(TASKS, dtype=jnp.int32)
    members = (task_of_token[:, None] == task_index[None, :]).astype(jnp.float32)
    task_counts = lax.psum(jnp.sum(members, axis=0), "dp")
    inverse = 1.0 / (TASKS * task_counts)
    weight = jnp.sum(members * inverse[None, :], axis=1)
    gathered = lax.all_gather(tokens, "dp", axis=0, tiled=True)
    linear_part = over_hidden(contract_last(gathered, up_weight))
    activation, derivative, second_order = sigmoid_parts(linear_part)
    hidden = activation.astype(jnp.bfloat16)

    def forward_term(first_row, slice_rows):
        return jnp.dot(hidden, down_weight, preferred_element_type=jnp.float32)

    output_rows = over_tokens(forward_term, row_count)
    errors = (weight[:, None] * (output_rows - targets.astype(jnp.float32))).astype(jnp.bfloat16)
    all_errors = all_tokens(errors)
    backward = over_hidden(contract_last(all_errors, down_weight)).astype(jnp.float32)

    def operator(vector_up, vector_down):
        direction_up = vector_up.astype(jnp.bfloat16)
        direction_down = vector_down.astype(jnp.bfloat16)
        tangent_linear = over_hidden(contract_last(gathered, direction_up)).astype(jnp.float32)
        tangent_hidden = (derivative * tangent_linear).astype(jnp.bfloat16)

        def tangent_term(first_row, slice_rows):
            return jnp.dot(
                tangent_hidden, down_weight, preferred_element_type=jnp.float32
            ) + jnp.dot(hidden, direction_down, preferred_element_type=jnp.float32)

        tangent_output = over_tokens(tangent_term, row_count)
        tangent_errors = (weight[:, None] * tangent_output).astype(jnp.bfloat16)
        gathered_tangent = all_tokens(tangent_errors)
        tangent_backward = over_hidden(
            contract_last(gathered_tangent, down_weight) + contract_last(all_errors, direction_down)
        )
        tangent_gate = (
            derivative * tangent_backward.astype(jnp.float32)
            + second_order * backward * tangent_linear
        ).astype(jnp.bfloat16)
        hessian_up = contract_first(tangent_gate, gathered)
        hessian_down = contract_first(tangent_hidden, all_errors) + contract_first(
            hidden, gathered_tangent
        )
        return (vector_up + hessian_up, vector_down + hessian_down)

    residual_up = outer_up.astype(jnp.float32)
    residual_down = outer_down.astype(jnp.float32)
    solution_up = jnp.zeros_like(residual_up)
    solution_down = jnp.zeros_like(residual_down)
    search_up, search_down = (residual_up, residual_down)
    image_up, image_down = operator(residual_up, residual_down)
    norm_now, product = both_totals(residual_up, residual_down, image_up, image_down)
    step_size = norm_now / product
    along_up, along_down = (image_up, image_down)
    for iteration in range(ITERS):
        solution_up = solution_up + step_size * search_up
        solution_down = solution_down + step_size * search_down
        residual_up = residual_up - step_size * along_up
        residual_down = residual_down - step_size * along_down
        if iteration + 1 < ITERS:
            image_up, image_down = operator(residual_up, residual_down)
            norm_next, product = both_totals(residual_up, residual_down, image_up, image_down)
            ratio_next = norm_next / norm_now
            step_size = norm_next / (product - ratio_next * norm_next / step_size)
            search_up = residual_up + ratio_next * search_up
            search_down = residual_down + ratio_next * search_down
            along_up = image_up + ratio_next * along_up
            along_down = image_down + ratio_next * along_down
            norm_now = norm_next
    return (solution_up, solution_down)


def solution(mesh):
    placed = (
        P("dp", "shard"),
        P("dp", "shard"),
        P("dp"),
        P("dp", "shard"),
        P("dp", "shard"),
        P("dp", "shard"),
        P("dp", "shard"),
    )
    return jax.shard_map(
        body,
        mesh=mesh,
        in_specs=placed,
        out_specs=(P("dp", "shard"), P("dp", "shard")),
        check_vma=False,
    )
```

profile of v0, /device:TPU:0, one launch (start us, length us, event | category | flops | bytes accessed | tf_op | source)
XLA Modules:
  0.0 610.7 jit_solution(8272210368168391806)
XLA Ops:
  7.2 32.7 %all_gather.30 = bf16[128,896]{1,0:T(8,128)(2,1)S(1)} all-gather(bf16[16,896]{1,0:T(8,128)(2,1)} %param.7), channel_id=1, replica_groups=mesh['dp'=8,'shard'=4] {'dp'}, dimensions={0}, use_global_device_ids=true | all-gather | bytes 258048 | tf_op jit(solution)/shard_map/all_gather | solution.py:71
  39.9 4.3 convolution_convert_fusion.2
  44.3 4.3 convolution_convert_fusion.1
  48.6 18.8 %reduce-scatter.10.cloned.1.call-done = bf16[128,592]{0,1:T(8,128)(2,1)} async-done(((bf16[128,2368]{0,1:T(8,128)(2,1)}), bf16[128,592]{0,1:T(8,128)(2,1)}) %reduce-scatter.10.cloned.1.call-update) | async-done | bytes 151568 | tf_op jit(solution)/shard_map/reduce_scatter | solution.py:31
  67.5 7.2 %all_gather.31 = bf16[128,2368]{0,1:T(8,128)(2,1)S(1)} all-gather(bf16[128,592]{0,1:T(8,128)(2,1)} %reduce-scatter.10.cloned.1.call-done), channel_id=1, replica_groups=mesh['dp'=8,'shard'=4] {'shard'}, dimensions={1}, use_global_device_ids=true | all-gather | bytes 757760 | tf_op jit(solution)/shard_map/all_gather | solution.py:34
  74.7 3.9 convolution_convert_fusion.3
  78.7 14.0 %reduce-scatter.12.cloned.1.call-done = bf16[128,592]{0,1:T(8,128)(2,1)} async-done(((bf16[128,2368]{0,1:T(8,128)(2,1)}), bf16[128,592]{0,1:T(8,128)(2,1)}) %reduce-scatter.12.cloned.1.call-update) | async-done | bytes 151568 | tf_op jit(solution)/shard_map/reduce_scatter | solution.py:31
  92.8 7.4 %all_gather.32 = bf16[128,2368]{0,1:T(8,128)(2,1)S(1)} all-gather(bf16[128,592]{0,1:T(8,128)(2,1)} %reduce-scatter.12.cloned.1.call-done), channel_id=1, replica_groups=mesh['dp'=8,'shard'=4] {'shard'}, dimensions={1}, use_global_device_ids=true | all-gather | bytes 757760 | tf_op jit(solution)/shard_map/all_gather | solution.py:34
  100.1 3.4 fusion.56
  103.6 1.7 fusion.43
  105.3 0.1 convert_reduce_fusion
  105.4 21.4 %psum.36 = f32[16]{0:T(128)S(1)} all-reduce(f32[16]{0:T(128)S(1)} %convert_reduce_fusion), channel_id=1, replica_groups=mesh['dp'=8,'shard'=4] {'dp'}, use_global_device_ids=true, to_apply=%region_5.0 | all-reduce | flops 16 | bytes 128 | tf_op jit(solution)/shard_map/psum | solution.py:68
  126.8 0.2 select_reduce_fusion
  127.0 24.9 %reduce-scatter.16.cloned.1.call-done = bf16[16,896]{1,0:T(8,128)(2,1)} async-done(((bf16[128,896]{1,0:T(8,128)(2,1)}), bf16[16,896]{1,0:T(8,128)(2,1)}) %reduce-scatter.16.cloned.1.call-update) | async-done | bytes 28688 | tf_op jit(solution)/shard_map/reduce_scatter | solution.py:38
  151.8 57.9 %reduce-scatter.14.cloned.1.call-done = bf16[16,896]{1,0:T(8,128)(2,1)} async-done(((bf16[128,896]{1,0:T(8,128)(2,1)}), bf16[16,896]{1,0:T(8,128)(2,1)}) %reduce-scatter.14.cloned.1.call-update) | async-done | bytes 28688 | tf_op jit(solution)/shard_map/reduce_scatter | solution.py:38
  209.8 0.8 multiply_convert_fusion.1
  210.6 30.7 %all_gather.34 = bf16[128,896]{1,0:T(8,128)(2,1)S(1)} all-gather(bf16[16,896]{1,0:T(8,128)(2,1)S(1)} %get-tuple-element.10), channel_id=1, replica_groups=mesh['dp'=8,'shard'=4] {'dp'}, dimensions={0}, use_global_device_ids=true | all-gather | bytes 258048 | tf_op jit(solution)/shard_map/all_gather | solution.py:47
  241.3 4.3 convolution_convert_fusion
  245.7 30.7 %all_gather.33 = bf16[128,896]{1,0:T(8,128)(2,1)S(1)} all-gather(bf16[16,896]{1,0:T(8,128)(2,1)S(1)} %get-tuple-element.11), channel_id=1, replica_groups=mesh['dp'=8,'shard'=4] {'dp'}, dimensions={0}, use_global_device_ids=true | all-gather | bytes 258048 | tf_op jit(solution)/shard_map/all_gather | solution.py:47
  276.4 3.6 fusion.71
  280.1 2.1 fusion.17
  282.2 0.2 reduce-scatter.22.cloned.1.call-start
  282.4 1.4 fusion.54
  283.8 7.1 %fusion.8 = (f32[]{:T(128)}, f32[]{:T(128)}, f32[2368,896]{1,0:T(8,128)}) fusion(bf16[2368,896]{1,0:T(8,128)(2,1)} %param.13, f32[2368,896]{1,0:T(8,128)S(1)} %fusion.54, bf16[128,896]{1,0:T(8,128)(2,1)S(1)} %all_gather.33, bf16[128,2368]{0,1:T(8,128)(2,1)S(1)} %all_gather.31), kind=kOutput, calls=%fused_computation.22 | convolution fusion | flops 559833088 | bytes 22052872 | tf_op jit(solution)/shard_map/dot_general | solution.py:25
  290.9 7.8 %all_gather.36 = bf16[128,2368]{0,1:T(8,128)(2,1)S(1)} all-gather(bf16[128,592]{0,1:T(8,128)(2,1)} %reduce-scatter.20.cloned.1.call-done), channel_id=1, replica_groups=mesh['dp'=8,'shard'=4] {'shard'}, dimensions={1}, use_global_device_ids=true | all-gather | bytes 757760 | tf_op jit(solution)/shard_map/all_gather | solution.py:34
  298.7 5.0 reduce-scatter.18.cloned.1.call-done
  303.7 7.2 %all_gather.35 = bf16[128,2368]{0,1:T(8,128)(2,1)S(1)} all-gather(bf16[128,592]{0,1:T(8,128)(2,1)} %reduce-scatter.18.cloned.1.call-done), channel_id=1, replica_groups=mesh['dp'=8,'shard'=4] {'shard'}, dimensions={1}, use_global_device_ids=true | all-gather | bytes 757760 | tf_op jit(solution)/shard_map/all_gather | solution.py:34
  311.0 7.7 %fusion.3 = (f32[]{:T(128)}, f32[]{:T(128)}, f32[2368,896]{1,0:T(8,128)}) fusion(bf16[2368,896]{1,0:T(8,128)(2,1)} %param.12, bf16[128,896]{1,0:T(8,128)(2,1)S(1)} %all_gather.30, bf16[128,2368]{0,1:T(8,128)(2,1)S(1)} %all_gather.32, bf16[128,2368]{0,1:T(8,128)(2,1)S(1)} %all_gather.35, bf16[128,2368]{0,1:T(8,128)(2,1)S(1)} %all_gather.36, ...), kind=kOutput, calls=%fused_computation.17 | convolution fusion | flops 562561024 | bytes 15384584 | tf_op jit(solution)/shard_map/dot_general | solution.py:25
  321.2 39.9 %all-reduce.1 = (f32[]{:T(128)}, f32[]{:T(128)}) all-reduce(f32[]{:T(128)S(6)} %add.97, f32[]{:T(128)S(6)} %add.107), channel_id=1, replica_groups=mesh['dp'=8,'shard'=4] {'dp','shard'}, use_global_device_ids=true, to_apply=%region_2.0 | all-reduce | flops 2 | bytes 16 | tf_op jit(solution)/shard_map/psum | solution.py:55
  362.3 7.0 %fusion.19 = bf16[128,2368]{0,1:T(8,128)(2,1)} fusion(bf16[128,896]{1,0:T(8,128)(2,1)S(1)} %all_gather.30, bf16[2368,896]{1,0:T(8,128)(2,1)} %param.12, f32[2368,896]{1,0:T(8,128)} %get-tuple-element.12, f32[]{:T(128)S(6)} %div.20), kind=kOutput, calls=%fused_computation.38 | convolution fusion | flops 554074112 | bytes 13565956 | tf_op jit(solution)/shard_map/dot_general | solution.py:19
  369.4 7.4 %multiply_reduce_fusion.1 = f32[]{:T(128)} fusion(f32[2368,896]{1,0:T(8,128)} %get-tuple-element.12, f32[]{:T(128)S(6)} %div.20, bf16[2368,896]{1,0:T(8,128)(2,1)} %param.12), kind=kLoop, calls=%fused_computation.27 | loop fusion | flops 12730367 | bytes 12730376 | tf_op jit(solution)/shard_map/reduce_sum | solution.py:51
  376.7 15.2 %reduce-scatter.22.cloned.1.call-done = bf16[128,592]{0,1:T(8,128)(2,1)} async-done(((bf16[128,2368]{0,1:T(8,128)(2,1)}), bf16[128,592]{0,1:T(8,128)(2,1)}) %reduce-scatter.22.cloned.1.call-update) | async-done | bytes 151568 | tf_op jit(solution)/shard_map/reduce_scatter | solution.py:31
  392.0 7.5 %all_gather.37 = bf16[128,2368]{0,1:T(8,128)(2,1)S(1)} all-gather(bf16[128,592]{0,1:T(8,128)(2,1)} %reduce-scatter.22.cloned.1.call-done), channel_id=1, replica_groups=mesh['dp'=8,'shard'=4] {'shard'}, dimensions={1}, use_global_device_ids=true | all-gather | bytes 757760 | tf_op jit(solution)/shard_map/all_gather | solution.py:34
  399.4 3.4 fusion.52
  402.8 7.1 %fusion.44 = bf16[128,896]{1,0:T(8,128)(2,1)} fusion(f32[128,896]{1,0:T(8,128)S(1)} %fusion.52, bf16[2368,896]{1,0:T(8,128)(2,1)} %param.13, f32[2368,896]{1,0:T(8,128)} %get-tuple-element.13, f32[]{:T(128)S(6)} %div.20, bf16[128,2368]{0,1:T(8,128)(2,1)S(1)} %all_gather.31), kind=kOutput, calls=%fused_computation.69 | convolution fusion | flops 553697280 | bytes 14024708 | tf_op jit(solution)/shard_map/dot_general | solution.py:93
  410.0 7.5 %multiply_reduce_fusion = f32[]{:T(128)} fusion(f32[2368,896]{1,0:T(8,128)} %get-tuple-element.13, f32[]{:T(128)S(6)} %div.20, bf16[2368,896]{1,0:T(8,128)(2,1)} %param.13), kind=kLoop, calls=%fused_computation.26 | loop fusion | flops 10608639 | bytes 12730376 | tf_op jit(solution)/shard_map/reduce_sum | solution.py:51
  418.6 47.3 %reduce-scatter.24.cloned.1.call-done = bf16[16,896]{1,0:T(8,128)(2,1)} async-done(((bf16[128,896]{1,0:T(8,128)(2,1)}), bf16[16,896]{1,0:T(8,128)(2,1)}) %reduce-scatter.24.cloned.1.call-update) | async-done | bytes 28688 | tf_op jit(solution)/shard_map/reduce_scatter | solution.py:38
  465.9 0.8 multiply_convert_fusion
  466.7 30.7 %all_gather.38 = bf16[128,896]{1,0:T(8,128)(2,1)S(1)} all-gather(bf16[16,896]{1,0:T(8,128)(2,1)S(1)} %multiply_convert_fusion), channel_id=1, replica_groups=mesh['dp'=8,'shard'=4] {'dp'}, dimensions={0}, use_global_device_ids=true | all-gather | bytes 258048 | tf_op jit(solution)/shard_map/all_gather | solution.py:47
  497.5 3.5 fusion.72
  500.9 6.9 %fusion.18 = bf16[128,2368]{0,1:T(8,128)(2,1)} fusion(f32[128,2368]{0,1:T(8,128)S(1)} %fusion.72, bf16[128,896]{1,0:T(8,128)(2,1)S(1)} %all_gather.34, bf16[2368,896]{1,0:T(8,128)(2,1)} %param.13, f32[2368,896]{1,0:T(8,128)} %get-tuple-element.13, f32[]{:T(128)S(6)} %div.20), kind=kOutput, calls=%fused_computation.37 | convolution fusion | flops 552255488 | bytes 14778372 | tf_op jit(solution)/shard_map/dot_general | solution.py:19
  507.8 1.4 fusion.50
  509.2 6.7 %fusion.1 = f32[]{:T(128)} fusion(f32[2368,896]{1,0:T(8,128)S(1)} %fusion.50, bf16[128,896]{1,0:T(8,128)(2,1)S(1)} %all_gather.38, f32[2368,896]{1,0:T(8,128)} %get-tuple-element.13, f32[]{:T(128)S(6)} %div.20, bf16[2368,896]{1,0:T(8,128)(2,1)} %param.13, bf16[128,2368]{0,1:T(8,128)(2,1)S(1)} %all_gather.31), kind=kOutput, calls=%fused_computation.15 | convolution fusion | flops 559833088 | bytes 22052872 | tf_op jit(solution)/shard_map/dot_general | solution.py:25
  515.9 13.5 %reduce-scatter.26.cloned.1.call-done = bf16[128,592]{0,1:T(8,128)(2,1)} async-done(((bf16[128,2368]{0,1:T(8,128)(2,1)}), bf16[128,592]{0,1:T(8,128)(2,1)}) %reduce-scatter.26.cloned.1.call-update) | async-done | bytes 151568 | tf_op jit(solution)/shard_map/reduce_scatter | solution.py:31
  529.3 7.5 %all_gather.39 = bf16[128,2368]{0,1:T(8,128)(2,1)S(1)} all-gather(bf16[128,592]{0,1:T(8,128)(2,1)} %reduce-scatter.26.cloned.1.call-done), channel_id=1, replica_groups=mesh['dp'=8,'shard'=4] {'shard'}, dimensions={1}, use_global_device_ids=true | all-gather | bytes 757760 | tf_op jit(solution)/shard_map/all_gather | solution.py:34
  536.8 7.0 %fusion = f32[]{:T(128)} fusion(bf16[128,896]{1,0:T(8,128)(2,1)S(1)} %all_gather.30, bf16[128,2368]{0,1:T(8,128)(2,1)S(1)} %all_gather.37, bf16[128,2368]{0,1:T(8,128)(2,1)S(1)} %all_gather.39, f32[2368,896]{1,0:T(8,128)} %get-tuple-element.12, f32[]{:T(128)S(6)} %div.20, bf16[2368,896]{1,0:T(8,128)(2,1)} %param.12, bf16[128,2368]{0,1:T(8,128)(2,1)S(1)} %all_gather.31, ...), kind=kOutput, calls=%fused_computation.14 | convolution fusion | flops 564682752 | bytes 15384584 | tf_op jit(solution)/shard_map/dot_general | solution.py:25
  545.0 39.9 %all-reduce = (f32[]{:T(128)}, f32[]{:T(128)}) all-reduce(f32[]{:T(128)S(6)} %add.108, f32[]{:T(128)S(6)} %add.115), channel_id=1, replica_groups=mesh['dp'=8,'shard'=4] {'dp','shard'}, use_global_device_ids=true, to_apply=%region_17.0 | all-reduce | flops 2 | bytes 16 | tf_op jit(solution)/shard_map/psum | solution.py:55
  589.3 14.8 %fusion.4 = (f32[2368,896]{1,0:T(8,128)}, f32[2368,896]{1,0:T(8,128)}) fusion(bf16[2368,896]{1,0:T(8,128)(2,1)} %param.12, f32[]{:T(128)S(6)} %div.21, f32[]{:T(128)S(6)} %div.23, f32[]{:T(128)S(6)} %div.20, f32[2368,896]{1,0:T(8,128)} %get-tuple-element.12, f32[2368,896]{1,0:T(8,128)} %get-tuple-element.13, bf16[2368,896]{1,0:T(8,128)(2,1)} %param.13), kind=kLoop, calls=%fused_computation.18 | loop fusion | flops 36069376 | bytes 42434572 | tf_op jit(solution)/shard_map/add | solution.py:121
  (33 shorter events, 0.5 us)
Async XLA Ops:
  7.2 60.3 %reduce-scatter.10.cloned.1.call-start = ((), (), s32[]{:S(2)}) async-start(), calls=%async_computation.9 | async-start | bytes 757760 | tf_op jit(solution)/shard_map/reduce_scatter | solution.py:31
  44.2 48.5 %reduce-scatter.12.cloned.1.call-start = ((), (), s32[]{:S(2)}) async-start(), calls=%async_computation.10 | async-start | bytes 757760 | tf_op jit(solution)/shard_map/reduce_scatter | solution.py:31
  48.6 103.2 %reduce-scatter.16.cloned.1.call-start = ((), (), s32[]{:S(2)}) async-start(), calls=%async_computation.12 | async-start | bytes 258048 | tf_op jit(solution)/shard_map/reduce_scatter | solution.py:38
  78.7 131.1 %reduce-scatter.14.cloned.1.call-start = ((), (), s32[]{:S(2)}) async-start(), calls=%async_computation.11 | async-start | bytes 258048 | tf_op jit(solution)/shard_map/reduce_scatter | solution.py:38
  92.8 10.8 %slice-start = ((s8[4243456]{0:T(1024)(128)(4,1)}), s8[4194304]{0:T(1024)(128)(4,1)S(1)}, s32[]{:S(2)}) async-start(s8[4243456]{0:T(1024)(128)(4,1)} %bitcast.26), calls=%async_computation.18 | async-start | bytes 8388608
  100.1 3.4 slice-start.1
  103.5 1.8 copy-start.1
  103.5 106.2 %copy-start = (bf16[16,896]{1,0:T(8,128)(2,1)S(1)}, bf16[16,896]{1,0:T(8,128)(2,1)}, u32[]{:S(2)}) copy-start(bf16[16,896]{1,0:T(8,128)(2,1)} %param.8) | copy-start | bytes 86020
  105.2 185.7 %reduce-scatter.20.cloned.1.call-start = ((), (), s32[]{:S(2)}) async-start(), calls=%async_computation.14 | async-start | bytes 757760 | tf_op jit(solution)/shard_map/reduce_scatter | solution.py:31
  245.6 34.4 %slice-start.2 = ((s8[4243456]{0:T(1024)(128)(4,1)}), s8[49152]{0:T(1024)(128)(4,1)S(1)}, s32[]{:S(2)}) async-start(s8[4243456]{0:T(1024)(128)(4,1)} %bitcast.28), calls=%async_computation.20 | async-start | bytes 98304
  245.7 58.1 %reduce-scatter.18.cloned.1.call-start = ((), (), s32[]{:S(2)}) async-start(), calls=%async_computation.13 | async-start | bytes 757760 | tf_op jit(solution)/shard_map/reduce_scatter | solution.py:31
  276.4 3.7 slice-start.3
  282.2 109.8 %reduce-scatter.22.cloned.1.call-start = ((), (), s32[]{:S(2)}) async-start(), calls=%async_computation.15 | async-start | bytes 757760 | tf_op jit(solution)/shard_map/reduce_scatter | solution.py:31
  369.3 96.6 %reduce-scatter.24.cloned.1.call-start = ((), (), s32[]{:S(2)}) async-start(), calls=%async_computation.16 | async-start | bytes 258048 | tf_op jit(solution)/shard_map/reduce_scatter | solution.py:38
  409.9 119.4 %reduce-scatter.26.cloned.1.call-start = ((), (), s32[]{:S(2)}) async-start(), calls=%async_computation.17 | async-start | bytes 757760 | tf_op jit(solution)/shard_map/reduce_scatter | solution.py:31
Sparse Core Ops, SparseCore 0:
  44.4 23.0 reduce-scatter.9
  70.6 22.1 reduce-scatter.11
  96.5 55.2 reduce-scatter.15
  155.4 54.3 reduce-scatter.13
  245.8 21.3 reduce-scatter.19
  282.3 21.3 reduce-scatter.17
  369.4 22.5 reduce-scatter.21
  410.1 55.8 reduce-scatter.23
  508.0 21.3 reduce-scatter.25
where the time goes:
time: 612 us; the launch traced here: 611 us
  blocking collectives  271 us (44%)
  waiting for transfers between devices  197 us (32%)
  matrix products  86.5 us (14%)
  other arithmetic  31.6 us (5%)
  between operations  24.6 us (4%)
    reduce_scatter x3, waiting for transfers between devices, over_tokens(): lax.psum_scatter(term_fn(jnp.int32(0), row_count * lax.axis_size('dp')).a...  130 us
    all_gather x3, blocking collectives, all_tokens(): return lax.all_gather(local_part, 'dp', axis=0, tiled=True)  92.1 us
    psum x2, blocking collectives, both_totals(): lax.psum((paired_sum(residual_up, residual_up, residual_down, residual_do...  79.7 us
    reduce_scatter x6, waiting for transfers between devices, over_hidden(): lax.psum_scatter(partial_value.astype(jnp.bfloat16), 'shard', scatter_dim...  66.6 us
    all_gather x6, blocking collectives, over_hidden(): return lax.all_gather(portion, 'shard', axis=1, tiled=True)  44.6 us
    dot_general x8, matrix products, contract_last(): lax.dot_general(left_side, right_side, (((1,), (1,)), ((), ())), preferre...  35.9 us
    all_gather x1, blocking collectives, body(): gathered = lax.all_gather(tokens, 'dp', axis=0, tiled=True)  32.7 us
    dot_general x6, matrix products, contract_first(): lax.dot_general(left_side, right_side, (((0,), (0,)), ((), ())), preferre...  31.2 us
  transfers between devices with their start and end apart: 9, of which 8 were waited for; matrix products, arithmetic and copies ran while one was open for 8% of the time, Pallas kernels for 0%

commit v1 on v0

v1 whole, which is shorter than its diff:
```python
import functools

import jax
import jax.numpy as jnp
from jax import lax
from jax.experimental import pallas as pl
from jax.experimental.pallas import tpu as pltpu
from jax.sharding import PartitionSpec as P

TASKS = 16
BF = jnp.bfloat16
F32 = jnp.float32
MESH = pl.DeviceIdType.MESH
VM = pl.BlockSpec(memory_space=pltpu.VMEM)


def sigmoid_parts(linear_part):
    argument = linear_part.astype(F32)
    logistic = jax.nn.sigmoid(argument)
    derivative = logistic * (1.0 + argument * (1.0 - logistic))
    second_order = logistic * (1.0 - logistic) * (2.0 + argument * (1.0 - 2.0 * logistic))
    return (argument * logistic, derivative, second_order)


def contract_last(left_side, right_side):
    return lax.dot_general(
        left_side, right_side, (((1,), (1,)), ((), ())), preferred_element_type=F32
    )


def contract_first(left_side, right_side):
    return lax.dot_general(
        left_side, right_side, (((0,), (0,)), ((), ())), preferred_element_type=F32
    )


def product(left_side, right_side):
    return jnp.dot(left_side, right_side, preferred_element_type=F32)


def remote(src, dst, send_sem, recv_sem, where):
    return pltpu.make_async_remote_copy(
        src_ref=src,
        dst_ref=dst,
        send_sem=send_sem,
        recv_sem=recv_sem,
        device_id=where,
        device_id_type=MESH,
    )


def greet(places):
    barrier = pltpu.get_barrier_semaphore()
    for place in places:
        pl.semaphore_signal(barrier, inc=1, device_id=place, device_id_type=MESH)
    pl.semaphore_wait(barrier, len(places))


def rows_at(index, count):
    return pl.ds(pl.multiple_of(index * count, count), count)


def call(kernel, outs, scratch, number, args):
    return pl.pallas_call(
        kernel,
        out_shape=outs,
        in_specs=[VM] * len(args),
        out_specs=[VM] * len(outs),
        scratch_shapes=scratch,
        compiler_params=pltpu.CompilerParams(
            collective_id=number, has_side_effects=True, vmem_limit_bytes=48 * 2**20
        ),
    )(*args)


def ring_places(axis, n):
    me = lax.axis_index(axis)
    return me, [{axis: lax.rem(me + k, n)} for k in range(1, n)], [
        lax.rem(me + k, n) for k in range(1, n)
    ]


def gather_kernel(n, count, *refs):
    ins, outs = refs[:count], refs[count : 2 * count]
    send_sem, recv_sem = refs[2 * count :]
    me, places, _ = ring_places("dp", n)
    for src, dst in zip(ins, outs):
        dst[rows_at(me, src.shape[0]), :] = src[...]
    greet(places)
    copies = []
    for k, place in enumerate(places):
        for i, (src, dst) in enumerate(zip(ins, outs)):
            rows = rows_at(me, src.shape[0])
            copies.append(
                remote(src, dst.at[rows, :], send_sem.at[i, k], recv_sem.at[i, k], place)
            )
            copies[-1].start()
    for copy in copies:
        copy.wait()


def gather_dp(n, number, *arrays):
    count = len(arrays)
    outs = [jax.ShapeDtypeStruct((n * a.shape[0], a.shape[1]), a.dtype) for a in arrays]
    sems = [pltpu.SemaphoreType.DMA((count, n - 1))] * 2
    return call(functools.partial(gather_kernel, n, count), outs, sems, number, arrays)


def sum_kernel(n, count, bits, *refs):
    ins, outs = refs[:count], refs[count : 2 * count]
    halves, accs, wires = (refs[(2 + j) * count : (3 + j) * count] for j in range(3))
    send_sem, recv_sem = refs[5 * count :]
    me = lax.axis_index("shard")

    def flip(bit):
        step = 1 << bit
        return {"shard": me + step - 2 * step * lax.rem(me // step, 2)}

    greet([flip(bit) for bit in range(bits)])
    low = lax.rem(me, 2)
    first = []
    for i in range(count):
        half = ins[i].shape[0] // 2
        first.append(
            remote(
                ins[i].at[rows_at(1 - low, half), :],
                halves[i],
                send_sem.at[i, 0],
                recv_sem.at[i, 0],
                flip(0),
            )
        )
        first[-1].start()
    now = []
    for i in range(count):
        half = ins[i].shape[0] // 2
        first[i].wait()
        total = ins[i][rows_at(low, half), :].astype(F32) + halves[i][...].astype(F32)
        accs[i][0] = total.astype(ins[i].dtype)
        if bits > 1:
            copy = remote(
                accs[i].at[0], wires[i].at[0], send_sem.at[i, 1], recv_sem.at[i, 1], flip(1)
            )
            copy.start()
            now.append(copy)
    last = []
    for i in range(count):
        half = ins[i].shape[0] // 2
        mine = rows_at(low, half)
        for bit in range(1, bits):
            now[i].wait()
            total = accs[i][bit - 1].astype(F32) + wires[i][bit - 1].astype(F32)
            accs[i][bit] = total.astype(ins[i].dtype)
            if bit + 1 < bits:
                now[i] = remote(
                    accs[i].at[bit],
                    wires[i].at[bit],
                    send_sem.at[i, bit + 1],
                    recv_sem.at[i, bit + 1],
                    flip(bit + 1),
                )
                now[i].start()
        outs[i][mine, :] = accs[i][bits - 1]
        copy = remote(
            accs[i].at[bits - 1],
            outs[i].at[mine, :],
            send_sem.at[i, bits],
            recv_sem.at[i, bits],
            flip(0),
        )
        copy.start()
        last.append(copy)
    for copy in last:
        copy.wait()


def sum_shard(n, number, *arrays):
    count = len(arrays)
    bits = n.bit_length() - 1
    outs = [jax.ShapeDtypeStruct(a.shape, a.dtype) for a in arrays]
    sizes = [(a.shape[0] // 2, a.shape[1]) for a in arrays]
    scratch = [pltpu.VMEM(s, a.dtype) for s, a in zip(sizes, arrays)]
    scratch += [pltpu.VMEM((bits,) + s, a.dtype) for s, a in zip(sizes, arrays)]
    scratch += [pltpu.VMEM((max(bits - 1, 1),) + s, a.dtype) for s, a in zip(sizes, arrays)]
    scratch += [pltpu.SemaphoreType.DMA((count, bits + 1))] * 2
    return call(functools.partial(sum_kernel, n, count, bits), outs, scratch, number, arrays)


def error_kernel(
    n, y_ref, z_ref, targets_ref, weight_ref, e_ref, t_ref, row_ref,
    held, fresh, send_sem, recv_sem, send_two, recv_two,
):
    rows = targets_ref.shape[0]
    me, places, peers = ring_places("dp", n)
    greet(places)
    copies = []
    for i, part in enumerate((y_ref, z_ref)):
        for k in range(n - 1):
            copy = remote(
                part.at[rows_at(peers[k], rows), :],
                held.at[i, k],
                send_sem.at[i, k],
                recv_sem.at[i, k],
                places[k],
            )
            copy.start()
            copies.append(copy)
    mine = rows_at(me, rows)
    weight = weight_ref[:, 0:1]
    second = []
    for i, part in enumerate((y_ref, z_ref)):
        total = part[mine, :].astype(F32)
        for k in range(n - 1):
            copies[i * (n - 1) + k].wait()
            total = total + held[i, k].astype(F32)
        if i == 0:
            value = (weight * (total - targets_ref[...].astype(F32))).astype(BF)
        else:
            row_ref[...] = total
            value = (weight * total).astype(BF)
        dst = (e_ref, t_ref)[i]
        fresh[i] = value
        dst[mine, :] = value
        for k in range(n - 1):
            copy = remote(
                fresh.at[i], dst.at[mine, :], send_two.at[i, k], recv_two.at[i, k], places[k]
            )
            copy.start()
            second.append(copy)
    for copy in second:
        copy.wait()


def all_errors(n, number, y, z, targets, weight):
    rows, width = targets.shape
    outs = [jax.ShapeDtypeStruct(y.shape, BF)] * 2 + [jax.ShapeDtypeStruct((rows, width), F32)]
    scratch = [pltpu.VMEM((2, n - 1, rows, width), BF), pltpu.VMEM((2, rows, width), BF)]
    scratch += [pltpu.SemaphoreType.DMA((2, n - 1))] * 4
    return call(
        functools.partial(error_kernel, n), outs, scratch, number, (y, z, targets, weight)
    )


def totals_kernel(
    n, m, w_ref, row_ref, weight_ref, part_ref, out_ref,
    held, dp_slots, shard_slots, own, send_sem, recv_sem, send_two, recv_two, send_three, recv_three,
):
    rows = row_ref.shape[0]
    me, places, peers = ring_places("dp", n)
    own_shard, shard_places, _ = ring_places("shard", m)
    greet(places + shard_places)
    copies = []
    for k in range(n - 1):
        copy = remote(
            w_ref.at[rows_at(peers[k], rows), :],
            held.at[k],
            send_sem.at[k],
            recv_sem.at[k],
            places[k],
        )
        copy.start()
        copies.append(copy)
    total = w_ref[rows_at(me, rows), :].astype(F32)
    for k in range(n - 1):
        copies[k].wait()
        total = total + held[k].astype(F32)
    row, weight = row_ref[...], weight_ref[:, 0:1]
    index = lax.broadcasted_iota(jnp.int32, part_ref.shape, 0)
    value = part_ref[...]
    for place, term in ((1, row * row), (3, row * total), (4, total * total)):
        number = jnp.sum(jnp.sum(weight * term, axis=1, keepdims=True), axis=0, keepdims=True)
        value = value + jnp.where(index == place, number, 0.0)
    own[0] = value
    dp_slots[pl.ds(me, 1)] = value[None]
    copies = []
    for k in range(n - 1):
        copy = remote(
            own.at[0], dp_slots.at[me], send_two.at[k], recv_two.at[k], places[k]
        )
        copy.start()
        copies.append(copy)
    for copy in copies:
        copy.wait()
    value = dp_slots[0]
    for k in range(1, n):
        value = value + dp_slots[k]
    own[1] = value
    shard_slots[pl.ds(own_shard, 1)] = value[None]
    copies = []
    for k in range(m - 1):
        copy = remote(
            own.at[1],
            shard_slots.at[own_shard],
            send_three.at[k],
            recv_three.at[k],
            shard_places[k],
        )
        copy.start()
        copies.append(copy)
    for copy in copies:
        copy.wait()
    value = shard_slots[0]
    for k in range(1, m):
        value = value + shard_slots[k]
    out_ref[...] = value


def all_totals(n, m, number, w, row, weight, part):
    scratch = [
        pltpu.VMEM((n - 1,) + row.shape, BF),
        pltpu.VMEM((n,) + part.shape, F32),
        pltpu.VMEM((m,) + part.shape, F32),
        pltpu.VMEM((2,) + part.shape, F32),
    ]
    scratch += [pltpu.SemaphoreType.DMA((n - 1,))] * 4 + [pltpu.SemaphoreType.DMA((m - 1,))] * 2
    outs = [jax.ShapeDtypeStruct(part.shape, F32)]
    return call(
        functools.partial(totals_kernel, n, m), outs, scratch, number, (w, row, weight, part)
    )[0]


def two_halves(matrix):
    high = matrix.astype(BF)
    return high, (matrix - high.astype(F32)).astype(BF)


def body(n, m, tokens, targets, task_of_token, up_weight, down_weight, outer_up, outer_down):
    rows = tokens.shape[0]
    count = rows * n
    task_block = jnp.broadcast_to(task_of_token.astype(F32)[:, None], (rows, 128))
    gathered, all_tasks = gather_dp(n, 0, tokens, task_block)
    same = (task_block[:, 0:1] == all_tasks[:, 0][None, :]).astype(F32)
    weight = 1.0 / (TASKS * jnp.sum(same, axis=1, keepdims=True))
    weight = jnp.broadcast_to(weight, (rows, 128))

    linear_part, tangent_linear = sum_shard(
        m,
        1,
        contract_last(gathered, up_weight).astype(BF),
        contract_last(gathered, outer_up).astype(BF),
    )
    activation, derivative, second_order = sigmoid_parts(linear_part)
    hidden = activation.astype(BF)
    tangent = tangent_linear.astype(F32)
    tangent_hidden = (derivative * tangent).astype(BF)

    both = product(jnp.concatenate([hidden, tangent_hidden], axis=0), down_weight)
    errors, tangent_errors, tangent_row = all_errors(
        n,
        2,
        both[:count].astype(BF),
        (both[count:] + product(hidden, outer_down)).astype(BF),
        targets,
        weight,
    )

    two_errors = jnp.concatenate([errors, tangent_errors], axis=0)
    back = contract_last(two_errors, down_weight)
    backward = back[:count]
    through_outer = contract_last(errors, outer_down)
    curved = second_order * backward
    gate_part = derivative * (back[count:] + through_outer) + curved * tangent
    token_gram = contract_last(gathered, gathered)
    tangent_gate, full_gram = sum_shard(m, 3, gate_part.astype(BF), token_gram)

    high, low = two_halves(full_gram)
    lowered = product(
        jnp.concatenate([high, low], axis=1),
        jnp.concatenate([tangent_gate, tangent_gate], axis=0),
    )
    carried = (derivative * lowered).astype(BF)
    hidden_gram = contract_last(
        jnp.concatenate([hidden, carried], axis=0),
        jnp.concatenate([tangent_hidden, hidden], axis=0),
    )
    tangent_gram = contract_last(tangent_hidden, tangent_hidden)
    hidden_tangent, hidden_hidden = hidden_gram[:count, :count], hidden_gram[:count, count:]
    carried_tangent, carried_hidden = hidden_gram[count:, :count], hidden_gram[count:, count:]
    error_gram = contract_last(two_errors, two_errors)
    error_error, error_tangent = error_gram[:count, :count], error_gram[:count, count:]
    further = product(carried, down_weight) + product(
        jnp.concatenate([hidden_tangent, hidden_hidden], axis=1).astype(BF), two_errors
    )

    start_norm = jnp.sum(jnp.square(outer_up.astype(F32))) + jnp.sum(
        jnp.square(outer_down.astype(F32))
    )
    crossing = through_outer
    first_term = jnp.sum(
        2.0 * tangent_hidden.astype(F32) * crossing + curved * tangent * tangent
    )
    mixed_term = jnp.sum(carried.astype(F32) * crossing + curved * tangent * lowered)
    last_term = jnp.sum(curved * lowered * lowered)
    gate_gram = contract_last(tangent_gate, tangent_gate)
    s_e = jnp.sum(tangent_gram * error_error)
    h_t = jnp.sum(hidden_tangent.T * error_tangent)
    change_norm = (
        jnp.sum(gate_gram * token_gram)
        + s_e
        + 2.0 * h_t
        + jnp.sum(hidden_hidden * error_gram[count:, count:])
    )
    mixed_term = mixed_term + s_e + h_t
    last_term = last_term + 2.0 * (
        jnp.sum(carried_tangent * error_error) + jnp.sum(carried_hidden * error_tangent)
    )
    index = lax.broadcasted_iota(jnp.int32, (8, 128), 0)
    part = jnp.zeros((8, 128), F32)
    for place, value in enumerate((start_norm, first_term, change_norm, mixed_term, last_term)):
        part = part + jnp.where(index == place, value, 0.0)

    sums = all_totals(n, m, 4, further.astype(BF), tangent_row, weight, part)
    norm, first, change, mixed, final = (sums[i, 0] for i in range(5))
    step = norm / (norm + first)
    keep = first / (norm + first)
    norm_next = keep * keep * norm - 2.0 * keep * step * first + step * step * change
    ratio = norm_next / norm
    curvature = (
        norm_next
        + keep * keep * first
        - 2.0 * keep * step * mixed
        + step * step * final
        - ratio * norm_next / step
    )
    step_next = norm_next / curvature
    of_outer = step + step_next * (ratio + keep)
    of_change = -step_next * step
    change_up = contract_first(tangent_gate, gathered)
    change_down = contract_first(
        jnp.concatenate([tangent_hidden, hidden], axis=0), two_errors
    )
    return (
        of_outer * outer_up.astype(F32) + of_change * change_up,
        of_outer * outer_down.astype(F32) + of_change * change_down,
    )


def solution(mesh):
    placed = tuple(P("dp") if i == 2 else P("dp", "shard") for i in range(7))
    return jax.shard_map(
        functools.partial(body, mesh.shape["dp"], mesh.shape["shard"]),
        mesh=mesh,
        in_specs=placed,
        out_specs=(P("dp", "shard"), P("dp", "shard")),
        check_vma=False,
    )
```

time: 612 us -> 158 us (0.26)
  blocking collectives: 271 us -> 0 us
  waiting for transfers between devices: 197 us -> 0 us
  Pallas kernels: 0 us -> 89.4 us
  matrix products: 86.5 us -> 40.4 us
  other arithmetic: 31.6 us -> 9.09 us
  between operations: 24.6 us -> 16 us
    reduce_scatter x9 -> x0, waiting for transfers between devices: 197 us -> none  [the longest x3 130 us: over_tokens(): lax.psum_scatter(term_fn(jnp.int32(0), row_count * lax.axis_size('dp')).a...]
    all_gather x10 -> x0, blocking collectives: 169 us -> none  [the longest x3 92.1 us: all_tokens(): return lax.all_gather(local_part, 'dp', axis=0, tiled=True)]
    psum x3 -> x0, blocking collectives: 101 us -> none  [the longest x2 79.7 us: both_totals(): lax.psum((paired_sum(residual_up, residual_up, residual_down, residual_do...]
    pallas_call x0 -> x5, Pallas kernels: none -> 89.4 us  [call(): pl.pallas_call(kernel, out_shape=outs, in_specs=[VM] * len(args), out_spe...]
    dot_general x8 -> x9, matrix products: 35.9 us -> 15.6 us  [contract_last(): lax.dot_general(left_side, right_side, (((1,), (1,)), ((), ())), preferre...]
    dot_general x6 -> x2, matrix products: 31.2 us -> 12 us  [contract_first(): lax.dot_general(left_side, right_side, (((0,), (0,)), ((), ())), preferre...]
    add x1, other arithmetic: 14.8 us -> 0.63 us  [body(): part = part + jnp.where(index == place, value, 0.0)]
    reduce_sum x4 -> x3, other arithmetic: 15.1 us -> 7.19 us  [the longest x1 6.29 us: body(): jnp.sum(jnp.square(outer_up.astype(F32)))]
  transfers between devices with their start and end apart: 9 -> 0, of which waited for: 8 -> 0; matrix products, arithmetic and copies ran while one was open for 8% -> 0% of each run, Pallas kernels for 0% -> 0%
where the time goes in v1:
time: 158 us; the launch traced here: 157 us
  Pallas kernels  89.4 us (57%)
  matrix products  40.4 us (26%)
  between operations  16 us (10%)
  other arithmetic  9.09 us (6%)
  local copies, waits for them, and re-layouts  2.57 us (2%)
    pallas_call x5, Pallas kernels, call(): pl.pallas_call(kernel, out_shape=outs, in_specs=[VM] * len(args), out_spe...  89.4 us
    dot_general x9, matrix products, contract_last(): lax.dot_general(left_side, right_side, (((1,), (1,)), ((), ())), preferre...  15.6 us
    dot_general x5, matrix products, product(): return jnp.dot(left_side, right_side, preferred_element_type=F32)  12.7 us
    dot_general x2, matrix products, contract_first(): lax.dot_general(left_side, right_side, (((0,), (0,)), ((), ())), preferre...  12 us
    reduce_sum x1, other arithmetic, body(): jnp.sum(jnp.square(outer_up.astype(F32)))  6.29 us

profile of v1, /device:TPU:0, one launch (start us, length us, event | category | flops | bytes accessed | tf_op | source)
XLA Modules:
  0.0 157.4 jit_solution(5992048983745449050)
XLA Ops:
  0.6 0.7 convert_element_type.61
  1.3 6.3 %fusion = (f32[]{:T(128)}, f32[]{:T(128)}) fusion(bf16[2368,896]{1,0:T(8,128)(2,1)} %param.12, bf16[2368,896]{1,0:T(8,128)(2,1)} %param.13), kind=kLoop, calls=%fused_computation.4 | loop fusion | flops 12730366 | bytes 8486920 | tf_op jit(solution)/shard_map/reduce_sum | solution.py:385
  8.9 0.1 broadcast_in_dim.36.refs_1_
  9.0 0.0 copy-done
  9.0 11.3 %shard_map.86 = (bf16[128,896]{1,0:T(8,128)(2,1)S(1)}, f32[128,128]{1,0:T(8,128)S(1)}) custom-call(bf16[16,896]{1,0:T(8,128)(2,1)S(1)} %copy-done, f32[16,128]{1,0:T(8,128)S(1)} %broadcast_in_dim.36.refs_1_), custom_call_target="tpu_custom_call" | custom-call | tf_op jit(solution)/shard_map/pallas_call | solution.py:64
  20.3 0.1 slice_reduce_fusion
  20.4 0.2 convert_reduce_fusion
  20.6 0.1 broadcast_in_dim.37.weight_ref
  20.7 0.2 fusion.51.refs_1_
  20.9 3.5 %convolution_convert_fusion = bf16[128,2368]{0,1:T(8,128)(2,1)S(1)} fusion(bf16[128,896]{1,0:T(8,128)(2,1)S(1)} %get-tuple-element.11, bf16[2368,896]{1,0:T(8,128)(2,1)} %param.12), kind=kOutput, calls=%fused_computation.8 | convolution fusion | flops 543465472 | bytes 5079040 | tf_op jit(solution)/shard_map/dot_general | solution.py:26
  24.4 0.3 copy.34.refs_1_
  24.7 3.5 %convolution_convert_fusion.1 = bf16[128,2368]{0,1:T(8,128)(2,1)S(1)} fusion(bf16[128,896]{1,0:T(8,128)(2,1)S(1)} %get-tuple-element.11, bf16[2368,896]{1,0:T(8,128)(2,1)} %param.10), kind=kOutput, calls=%fused_computation.9 | convolution fusion | flops 543465472 | bytes 5079040 | tf_op jit(solution)/shard_map/dot_general | solution.py:26
  28.2 0.3 copy.33.refs_0_
  28.5 19.4 %shard_map.87 = (bf16[128,2368]{1,0:T(8,128)(2,1)S(1)}, bf16[128,2368]{1,0:T(8,128)(2,1)S(1)}) custom-call(bf16[128,2368]{1,0:T(8,128)(2,1)S(1)} %copy.33.refs_0_, bf16[128,2368]{1,0:T(8,128)(2,1)S(1)} %copy.34.refs_1_), custom_call_target="tpu_custom_call" | custom-call | tf_op jit(solution)/shard_map/pallas_call | solution.py:64
  47.9 0.0 slice-start.2
  48.0 0.6 fusion.8
  48.6 0.0 copy-start.2
  48.6 0.8 copy-done.2
  49.4 3.8 %fusion.4 = f32[256,896]{1,0:T(8,128)S(1)} fusion(bf16[2368,896]{1,0:T(8,128)(2,1)} %param.11, bf16[128,2368]{1,0:T(8,128)(2,1)S(1)} %get-tuple-element.31, bf16[128,2368]{1,0:T(8,128)(2,1)S(1)} %get-tuple-element.30), kind=kOutput, calls=%fused_computation.21 | convolution fusion | flops 1088749568 | bytes 6373376 | tf_op jit(solution)/shard_map/dot_general | solution.py:38
  53.2 0.0 slice-done.2
  53.3 0.0 copy-start.1
  53.3 0.0 slice-start.5
  53.3 0.9 fusion.28.z_ref
  54.3 26.7 %shard_map.88 = (bf16[128,896]{1,0:T(8,128)(2,1)S(1)}, bf16[128,896]{1,0:T(8,128)(2,1)S(1)}, f32[16,896]{1,0:T(8,128)S(1)}) custom-call(bf16[128,896]{1,0:T(8,128)(2,1)S(1)} %slice.116.y_ref, bf16[128,896]{1,0:T(8,128)(2,1)S(1)} %fusion.28.z_ref, bf16[16,896]{1,0:T(8,128)(2,1)S(1)} %copy-done.1, f32[16,128]{1,0:T(8,128)S(1)} %broadcast_in_dim.37.weight_ref), custom_call_target="tpu_custom_call" | custom-call | tf_op jit(solution)/shard_map/pallas_call | solution.py:64
  81.1 0.3 fusion.52
  81.4 0.9 fusion.31
  82.4 1.5 fusion.50
  83.9 0.0 copy-start.4
  83.9 2.6 %fusion.21 = (bf16[128,2368]{1,0:T(8,128)(2,1)S(1)}, f32[128,2368]{1,0:T(8,128)}) fusion(f32[256,2368]{1,0:T(8,128)S(1)} %fusion.50, bf16[128,2368]{1,0:T(8,128)(2,1)S(1)} %get-tuple-element.13, bf16[128,2368]{1,0:T(8,128)(2,1)S(1)} %get-tuple-element.12, bf16[128,896]{1,0:T(8,128)(2,1)S(1)} %get-tuple-element.15, bf16[2368,896]{1,0:T(8,128)(2,1)S(1)} %bitcast.36), kind=kOutput, calls=%fused_computation.39 | convolution fusion | flops 549527552 | bytes 9928704 | tf_op jit(solution)/shard_map/dot_general | solution.py:26
  86.6 13.1 %shard_map.89 = (bf16[128,2368]{1,0:T(8,128)(2,1)S(1)}, f32[128,128]{1,0:T(8,128)S(1)}) custom-call(bf16[128,2368]{1,0:T(8,128)(2,1)S(1)} %get-tuple-element.37.refs_0_, f32[128,128]{1,0:T(8,128)S(1)} %fusion.51.refs_1_), custom_call_target="tpu_custom_call" | custom-call | tf_op jit(solution)/shard_map/pallas_call | solution.py:64
  99.7 1.0 fusion.30
  101.9 4.6 %fusion.10 = (f32[]{:T(128)}, f32[]{:T(128)}, f32[]{:T(128)}, bf16[128,2368]{1,0:T(8,128)(2,1)}) fusion(bf16[128,2368]{1,0:T(8,128)(2,1)S(1)} %get-tuple-element.13, f32[128,2368]{1,0:T(8,128)} %get-tuple-element.38, bf16[128,2368]{1,0:T(8,128)(2,1)S(1)} %get-tuple-element.30, f32[256,2368]{1,0:T(8,128)} %copy-done.4, ...), kind=kOutput, calls=%fused_computation.27 | convolution fusion | flops 167747584 | bytes 5521420 | tf_op jit(solution)/shard_map/dot_general | solution.py:38
  107.6 2.0 %fusion.5 = f32[256,256]{1,0:T(8,128)S(1)} fusion(bf16[128,2368]{1,0:T(8,128)(2,1)} %copy-done.2, bf16[128,2368]{1,0:T(8,128)(2,1)} %get-tuple-element.27, bf16[128,2368]{1,0:T(8,128)(2,1)S(1)} %get-tuple-element.30), kind=kOutput, calls=%fused_computation.22 | convolution fusion | flops 315228160 | bytes 2080768 | tf_op jit(solution)/shard_map/dot_general | solution.py:26
  109.7 0.1 copy.48
  109.8 0.7 fusion.35
  114.4 0.6 fusion.43
  115.0 0.1 iota.19.part_ref
  115.1 0.2 fusion.32
  115.4 0.0 copy-done.7
  115.4 0.0 copy-start.3
  115.4 0.0 slice-start
  115.4 3.1 %fusion.29.w_ref = bf16[128,896]{1,0:T(8,128)(2,1)S(1)} fusion(f32[128,896]{1,0:T(8,128)S(1)} %fusion.32, bf16[128,2368]{1,0:T(8,128)(2,1)S(1)} %copy-done.7, bf16[2368,896]{1,0:T(8,128)(2,1)} %param.11), kind=kOutput, calls=%fused_computation.52 | convolution fusion | flops 543391744 | bytes 5537792 | tf_op jit(solution)/shard_map/dot_general | solution.py:38
  118.5 18.7 %shard_map.90 = f32[8,128]{1,0:T(8,128)S(1)} custom-call(bf16[128,896]{1,0:T(8,128)(2,1)S(1)} %fusion.29.w_ref, f32[16,896]{1,0:T(8,128)S(1)} %get-tuple-element.19.row_ref, f32[16,128]{1,0:T(8,128)S(1)} %broadcast_in_dim.37.weight_ref, f32[8,128]{1,0:T(8,128)S(1)} %iota.19.part_ref), custom_call_target="tpu_custom_call" | custom-call | tf_op jit(solution)/shard_map/pallas_call | solution.py:64
  137.2 0.6 fusion.49
  145.3 0.0 copy-done.3
  145.3 0.0 slice-start.1
  145.3 7.3 %fusion.3 = f32[2368,896]{1,0:T(8,128)} fusion(bf16[2368,896]{1,0:T(8,128)(2,1)} %param.13, bf16[256,896]{1,0:T(8,128)(2,1)S(1)} %constant_dynamic-update-slice_fusion, f32[]{:T(128)S(6)} %mul.196, f32[]{:T(128)S(6)} %add.117, bf16[128,2368]{1,0:T(8,128)(2,1)S(1)} %copy-done.3, bf16[128,2368]{1,0:T(8,128)(2,1)S(1)} %get-tuple-element.30), kind=kOutput, calls=%fused_computation.7 | convolution fusion | flops 1097236480 | bytes 14401544 | tf_op jit(solution)/shard_map/dot_general | solution.py:32
  152.6 4.8 %fusion.1 = f32[2368,896]{1,0:T(8,128)} fusion(bf16[2368,896]{1,0:T(8,128)(2,1)S(1)} %bitcast.34, bf16[128,2368]{1,0:T(8,128)(2,1)S(1)} %get-tuple-element.18, bf16[128,896]{1,0:T(8,128)(2,1)S(1)} %get-tuple-element.11, f32[]{:T(128)S(6)} %mul.196, f32[]{:T(128)S(6)} %add.117), kind=kOutput, calls=%fused_computation.5 | convolution fusion | flops 551649280 | bytes 13565960 | tf_op jit(solution)/shard_map/dot_general | solution.py:32
  (24 shorter events, 0.1 us)
Async XLA Ops:
  1.3 7.7 %copy-start = (bf16[16,896]{1,0:T(8,128)(2,1)S(1)}, bf16[16,896]{1,0:T(8,128)(2,1)}, u32[]{:S(2)}) copy-start(bf16[16,896]{1,0:T(8,128)(2,1)} %refs_0_.1) | copy-start | bytes 86020
  47.9 5.3 %slice-start.2 = ((s8[4243456]{0:T(1024)(128)(4,1)}), s8[4194304]{0:T(1024)(128)(4,1)S(1)}, s32[]{:S(2)}) async-start(s8[4243456]{0:T(1024)(128)(4,1)} %bitcast.35), calls=%async_computation.2 | async-start | bytes 8388608
  48.6 0.8 copy-start.2
  49.4 3.9 %slice-start.3 = ((s8[4243456]{0:T(1024)(128)(4,1)}), s8[49152]{0:T(1024)(128)(4,1)S(1)}, s32[]{:S(2)}) async-start(s8[4243456]{0:T(1024)(128)(4,1)} %bitcast.35), calls=%async_computation.3 | async-start | bytes 98304
  49.4 33.0 %slice-start.4 = ((s8[4243456]{0:T(1024)(128)(4,1)}), s8[4194304]{0:T(1024)(128)(4,1)S(1)}, s32[]{:S(2)}) async-start(s8[4243456]{0:T(1024)(128)(4,1)} %bitcast.37), calls=%async_computation.4 | async-start | bytes 8388608
  53.3 1.0 copy-start.1
  53.3 29.1 %slice-start.5 = ((s8[4243456]{0:T(1024)(128)(4,1)}), s8[49152]{0:T(1024)(128)(4,1)S(1)}, s32[]{:S(2)}) async-start(s8[4243456]{0:T(1024)(128)(4,1)} %bitcast.37), calls=%async_computation.5 | async-start | bytes 98304
  81.4 2.5 %copy-start.5 = (f32[256,256]{1,0:T(8,128)}, f32[256,256]{1,0:T(8,128)S(1)}, u32[]{:S(2)}) copy-start(f32[256,256]{1,0:T(8,128)S(1)} %fusion.52) | copy-start | bytes 786436
  83.9 2.6 %copy-start.4 = (f32[256,2368]{1,0:T(8,128)}, f32[256,2368]{1,0:T(8,128)S(1)}, u32[]{:S(2)}) copy-start(f32[256,2368]{1,0:T(8,128)S(1)} %fusion.50) | copy-start | bytes 7274500
  107.6 2.2 %copy-start.6 = (f32[256,256]{1,0:T(8,128)S(1)}, f32[256,256]{1,0:T(8,128)}, u32[]{:S(2)}) copy-start(f32[256,256]{1,0:T(8,128)} %copy-done.5) | copy-start | bytes 786436
  109.7 5.7 %copy-start.7 = (bf16[128,2368]{1,0:T(8,128)(2,1)S(1)}, bf16[128,2368]{1,0:T(8,128)(2,1)}, u32[]{:S(2)}) copy-start(bf16[128,2368]{1,0:T(8,128)(2,1)} %get-tuple-element.27) | copy-start | bytes 1818628
  115.4 30.0 %copy-start.3 = (bf16[128,2368]{1,0:T(8,128)(2,1)S(1)}, bf16[128,2368]{1,0:T(8,128)(2,1)}, u32[]{:S(2)}) copy-start(bf16[128,2368]{1,0:T(8,128)(2,1)} %copy-done.2) | copy-start | bytes 1818628
  115.4 37.2 %slice-start = ((s8[4243456]{0:T(1024)(128)(4,1)}), s8[49152]{0:T(1024)(128)(4,1)S(1)}, s32[]{:S(2)}) async-start(s8[4243456]{0:T(1024)(128)(4,1)} %bitcast.33), calls=%async_computation | async-start | bytes 98304
  145.3 7.3 %slice-start.1 = ((s8[4243456]{0:T(1024)(128)(4,1)}), s8[4194304]{0:T(1024)(128)(4,1)S(1)}, s32[]{:S(2)}) async-start(s8[4243456]{0:T(1024)(128)(4,1)} %bitcast.33), calls=%async_computation.1 | async-start | bytes 8388608

commit v2 on v1

--- a/solution.py
+++ b/solution.py
@@ -60,11 +60,11 @@
     return pl.ds(pl.multiple_of(index * count, count), count)
 
 
-def call(kernel, outs, scratch, number, args):
+def call(kernel, outs, scratch, number, args, far=0):
     return pl.pallas_call(
         kernel,
         out_shape=outs,
-        in_specs=[VM] * len(args),
+        in_specs=[pl.BlockSpec(memory_space=pl.ANY)] * far + [VM] * (len(args) - far),
         out_specs=[VM] * len(outs),
         scratch_shapes=scratch,
         compiler_params=pltpu.CompilerParams(
@@ -80,9 +80,17 @@
     ]
 
 
-def gather_kernel(n, count, *refs):
-    ins, outs = refs[:count], refs[count : 2 * count]
-    send_sem, recv_sem = refs[2 * count :]
+def gather_kernel(
+    n, count, up_ref, down_ref, *refs
+):
+    ins, outs, norm_ref = refs[:count], refs[count : 2 * count], refs[2 * count]
+    held, load_sem, send_sem, recv_sem = refs[2 * count + 1 :]
+    loads = [
+        pltpu.make_async_copy(src, held.at[i], load_sem.at[i])
+        for i, src in enumerate((up_ref, down_ref))
+    ]
+    for load in loads:
+        load.start()
     me, places, _ = ring_places("dp", n)
     for src, dst in zip(ins, outs):
         dst[rows_at(me, src.shape[0]), :] = src[...]
@@ -95,15 +103,31 @@
                 remote(src, dst.at[rows, :], send_sem.at[i, k], recv_sem.at[i, k], place)
             )
             copies[-1].start()
+    size, width = up_ref.shape
+    total = jnp.zeros((16, width), F32)
+    for i, load in enumerate(loads):
+        load.wait()
+
+        def add(step, value, i=i):
+            block = held[i, rows_at(step, 16), :].astype(F32)
+            return value + block * block
+
+        total = lax.fori_loop(0, size // 16, add, total)
+    number = jnp.sum(jnp.sum(total, axis=1, keepdims=True), axis=0, keepdims=True)
+    norm_ref[...] = jnp.broadcast_to(number, norm_ref.shape)
     for copy in copies:
         copy.wait()
 
 
-def gather_dp(n, number, *arrays):
+def gather_dp(n, number, up, down, *arrays):
     count = len(arrays)
     outs = [jax.ShapeDtypeStruct((n * a.shape[0], a.shape[1]), a.dtype) for a in arrays]
-    sems = [pltpu.SemaphoreType.DMA((count, n - 1))] * 2
-    return call(functools.partial(gather_kernel, n, count), outs, sems, number, arrays)
+    outs.append(jax.ShapeDtypeStruct((8, 128), F32))
+    scratch = [pltpu.VMEM((2,) + up.shape, up.dtype), pltpu.SemaphoreType.DMA((2,))]
+    scratch += [pltpu.SemaphoreType.DMA((count, n - 1))] * 2
+    return call(
+        functools.partial(gather_kernel, n, count), outs, scratch, number, (up, down) + arrays, 2
+    )
 
 
 def sum_kernel(n, count, bits, *refs):
@@ -242,7 +266,8 @@
 
 
 def totals_kernel(
-    n, m, w_ref, row_ref, weight_ref, part_ref, out_ref,
+    n, m, w_ref, row_ref, weight_ref, part_ref, norm_ref, hidden_ref, tangent_ref, gate_ref,
+    token_ref, error_ref, out_ref,
     held, dp_slots, shard_slots, own, send_sem, recv_sem, send_two, recv_two, send_three, recv_three,
 ):
     rows = row_ref.shape[0]
@@ -260,6 +285,20 @@
         )
         copy.start()
         copies.append(copy)
+    count = gate_ref.shape[0]
+
+    def summed(term):
+        return jnp.sum(jnp.sum(term, axis=1, keepdims=True), axis=0, keepdims=True)
+
+    head, tail = pl.ds(0, count), pl.ds(count, count)
+    errors, crossed = error_ref[head, head], error_ref[tail, head]
+    tangents = tangent_ref[...]
+    s_e = summed(tangents * errors)
+    h_t = summed(hidden_ref[head, head] * crossed)
+    change = summed(gate_ref[...] * token_ref[...]) + s_e + 2.0 * h_t
+    change = change + summed(hidden_ref[head, tail] * error_ref[tail, tail])
+    carry = summed(hidden_ref[tail, head] * errors)
+    carry = carry + summed(hidden_ref[tail, tail] * error_ref[head, tail])
     total = w_ref[rows_at(me, rows), :].astype(F32)
     for k in range(n - 1):
         copies[k].wait()
@@ -267,8 +306,11 @@
     row, weight = row_ref[...], weight_ref[:, 0:1]
     index = lax.broadcasted_iota(jnp.int32, part_ref.shape, 0)
     value = part_ref[...]
+    for place, number in ((2, change), (3, s_e + h_t), (4, 2.0 * carry)):
+        value = value + jnp.where(index == place, number, 0.0)
+    value = value + jnp.where(index == 0, norm_ref[...], 0.0)
     for place, term in ((1, row * row), (3, row * total), (4, total * total)):
-        number = jnp.sum(jnp.sum(weight * term, axis=1, keepdims=True), axis=0, keepdims=True)
+        number = summed(weight * term)
         value = value + jnp.where(index == place, number, 0.0)
     own[0] = value
     dp_slots[pl.ds(me, 1)] = value[None]
@@ -302,115 +344,8 @@
     value = shard_slots[0]
     for k in range(1, m):
         value = value + shard_slots[k]
-    out_ref[...] = value
-
-
-def all_totals(n, m, number, w, row, weight, part):
-    scratch = [
-        pltpu.VMEM((n - 1,) + row.shape, BF),
-        pltpu.VMEM((n,) + part.shape, F32),
-        pltpu.VMEM((m,) + part.shape, F32),
-        pltpu.VMEM((2,) + part.shape, F32),
-    ]
-    scratch += [pltpu.SemaphoreType.DMA((n - 1,))] * 4 + [pltpu.SemaphoreType.DMA((m - 1,))] * 2
-    outs = [jax.ShapeDtypeStruct(part.shape, F32)]
-    return call(
-        functools.partial(totals_kernel, n, m), outs, scratch, number, (w, row, weight, part)
-    )[0]
-
-
-def two_halves(matrix):
-    high = matrix.astype(BF)
-    return high, (matrix - high.astype(F32)).astype(BF)
-
-
-def body(n, m, tokens, targets, task_of_token, up_weight, down_weight, outer_up, outer_down):
-    rows = tokens.shape[0]
-    count = rows * n
-    task_block = jnp.broadcast_to(task_of_token.astype(F32)[:, None], (rows, 128))
-    gathered, all_tasks = gather_dp(n, 0, tokens, task_block)
-    same = (task_block[:, 0:1] == all_tasks[:, 0][None, :]).astype(F32)
-    weight = 1.0 / (TASKS * jnp.sum(same, axis=1, keepdims=True))
-    weight = jnp.broadcast_to(weight, (rows, 128))
-
-    linear_part, tangent_linear = sum_shard(
-        m,
-        1,
-        contract_last(gathered, up_weight).astype(BF),
-        contract_last(gathered, outer_up).astype(BF),
-    )
-    activation, derivative, second_order = sigmoid_parts(linear_part)
-    hidden = activation.astype(BF)
-    tangent = tangent_linear.astype(F32)
-    tangent_hidden = (derivative * tangent).astype(BF)
-
-    both = product(jnp.concatenate([hidden, tangent_hidden], axis=0), down_weight)
-    errors, tangent_errors, tangent_row = all_errors(
-        n,
-        2,
-        both[:count].astype(BF),
-        (both[count:] + product(hidden, outer_down)).astype(BF),
-        targets,
-        weight,
-    )
-
-    two_errors = jnp.concatenate([errors, tangent_errors], axis=0)
-    back = contract_last(two_errors, down_weight)
-    backward = back[:count]
-    through_outer = contract_last(errors, outer_down)
-    curved = second_order * backward
-    gate_part = derivative * (back[count:] + through_outer) + curved * tangent
-    token_gram = contract_last(gathered, gathered)
-    tangent_gate, full_gram = sum_shard(m, 3, gate_part.astype(BF), token_gram)
-
-    high, low = two_halves(full_gram)
-    lowered = product(
-        jnp.concatenate([high, low], axis=1),
-        jnp.concatenate([tangent_gate, tangent_gate], axis=0),
-    )
-    carried = (derivative * lowered).astype(BF)
-    hidden_gram = contract_last(
-        jnp.concatenate([hidden, carried], axis=0),
-        jnp.concatenate([tangent_hidden, hidden], axis=0),
-    )
-    tangent_gram = contract_last(tangent_hidden, tangent_hidden)
-    hidden_tangent, hidden_hidden = hidden_gram[:count, :count], hidden_gram[:count, count:]
-    carried_tangent, carried_hidden = hidden_gram[count:, :count], hidden_gram[count:, count:]
-    error_gram = contract_last(two_errors, two_errors)
-    error_error, error_tangent = error_gram[:count, :count], error_gram[:count, count:]
-    further = product(carried, down_weight) + product(
-        jnp.concatenate([hidden_tangent, hidden_hidden], axis=1).astype(BF), two_errors
-    )
-
-    start_norm = jnp.sum(jnp.square(outer_up.astype(F32))) + jnp.sum(
-        jnp.square(outer_down.astype(F32))
-    )
-    crossing = through_outer
-    first_term = jnp.sum(
-        2.0 * tangent_hidden.astype(F32) * crossing + curved * tangent * tangent
-    )
-    mixed_term = jnp.sum(carried.astype(F32) * crossing + curved * tangent * lowered)
-    last_term = jnp.sum(curved * lowered * lowered)
-    gate_gram = contract_last(tangent_gate, tangent_gate)
-    s_e = jnp.sum(tangent_gram * error_error)
-    h_t = jnp.sum(hidden_tangent.T * error_tangent)
-    change_norm = (
-        jnp.sum(gate_gram * token_gram)
-        + s_e
-        + 2.0 * h_t
-        + jnp.sum(hidden_hidden * error_gram[count:, count:])
-    )
-    mixed_term = mixed_term + s_e + h_t
-    last_term = last_term + 2.0 * (
-        jnp.sum(carried_tangent * error_error) + jnp.sum(carried_hidden * error_tangent)
-    )
-    index = lax.broadcasted_iota(jnp.int32, (8, 128), 0)
-    part = jnp.zeros((8, 128), F32)
-    for place, value in enumerate((start_norm, first_term, change_norm, mixed_term, last_term)):
-        part = part + jnp.where(index == place, value, 0.0)
-
-    sums = all_totals(n, m, 4, further.astype(BF), tangent_row, weight, part)
-    norm, first, change, mixed, final = (sums[i, 0] for i in range(5))
+    own[2] = value
+    norm, first, change, mixed, final = (own[2, i : i + 1, :] for i in range(5))
     step = norm / (norm + first)
     keep = first / (norm + first)
     norm_next = keep * keep * norm - 2.0 * keep * step * first + step * step * change
@@ -423,8 +358,112 @@
         - ratio * norm_next / step
     )
     step_next = norm_next / curvature
-    of_outer = step + step_next * (ratio + keep)
-    of_change = -step_next * step
+    out_ref[0:1, :] = step + step_next * (ratio + keep)
+    out_ref[1:2, :] = -step_next * step
+
+
+def all_totals(n, m, number, w, row, weight, part, *others):
+    scratch = [
+        pltpu.VMEM((n - 1,) + row.shape, BF),
+        pltpu.VMEM((n,) + part.shape, F32),
+        pltpu.VMEM((m,) + part.shape, F32),
+        pltpu.VMEM((3,) + part.shape, F32),
+    ]
+    scratch += [pltpu.SemaphoreType.DMA((n - 1,))] * 4 + [pltpu.SemaphoreType.DMA((m - 1,))] * 2
+    outs = [jax.ShapeDtypeStruct((2, 128), F32)]
+    return call(
+        functools.partial(totals_kernel, n, m), outs, scratch, number, (w, row, weight, part) + others
+    )[0]
+
+
+def two_halves(matrix):
+    high = matrix.astype(BF)
+    return high, (matrix - high.astype(F32)).astype(BF)
+
+
+def body(n, m, tokens, targets, task_of_token, up_weight, down_weight, outer_up, outer_down):
+    rows = tokens.shape[0]
+    count = rows * n
+    task_block = jnp.broadcast_to(task_of_token.astype(F32)[:, None], (rows, 128))
+    gathered, all_tasks, start_norm = gather_dp(n, 0, outer_up, outer_down, tokens, task_block)
+    same = (task_block[:, 0:1] == all_tasks[:, 0][None, :]).astype(F32)
+    weight = 1.0 / (TASKS * jnp.sum(same, axis=1, keepdims=True))
+    weight = jnp.broadcast_to(weight, (rows, 128))
+
+    linear_part, tangent_linear = sum_shard(
+        m,
+        1,
+        contract_last(gathered, up_weight).astype(BF),
+        contract_last(gathered, outer_up).astype(BF),
+    )
+    activation, derivative, second_order = sigmoid_parts(linear_part)
+    hidden = activation.astype(BF)
+    tangent = tangent_linear.astype(F32)
+    tangent_hidden = (derivative * tangent).astype(BF)
+
+    both = product(jnp.concatenate([hidden, tangent_hidden], axis=0), down_weight)
+    errors, tangent_errors, tangent_row = all_errors(
+        n,
+        2,
+        both[:count].astype(BF),
+        (both[count:] + product(hidden, outer_down)).astype(BF),
+        targets,
+        weight,
+    )
+
+    two_errors = jnp.concatenate([errors, tangent_errors], axis=0)
+    back = contract_last(two_errors, down_weight)
+    backward = back[:count]
+    through_outer = contract_last(errors, outer_down)
+    curved = second_order * backward
+    gate_part = derivative * (back[count:] + through_outer) + curved * tangent
+    token_gram = contract_last(gathered, gathered)
+    tangent_gate, full_gram = sum_shard(m, 3, gate_part.astype(BF), token_gram)
+
+    high, low = two_halves(full_gram)
+    lowered = product(
+        jnp.concatenate([high, low], axis=1),
+        jnp.concatenate([tangent_gate, tangent_gate], axis=0),
+    )
+    carried = (derivative * lowered).astype(BF)
+    hidden_gram = contract_last(
+        jnp.concatenate([hidden, carried], axis=0),
+        jnp.concatenate([tangent_hidden, hidden], axis=0),
+    )
+    tangent_gram = contract_last(tangent_hidden, tangent_hidden)
+    error_gram = contract_last(two_errors, two_errors)
+    further = product(carried, down_weight) + product(
+        hidden_gram[:count].astype(BF), two_errors
+    )
+
+    crossing = through_outer
+    first_term = jnp.sum(
+        2.0 * tangent_hidden.astype(F32) * crossing + curved * tangent * tangent
+    )
+    mixed_term = jnp.sum(carried.astype(F32) * crossing + curved * tangent * lowered)
+    last_term = jnp.sum(curved * lowered * lowered)
+    gate_gram = contract_last(tangent_gate, tangent_gate)
+    index = lax.broadcasted_iota(jnp.int32, (8, 128), 0)
+    part = jnp.zeros((8, 128), F32)
+    for place, value in ((1, first_term), (3, mixed_term), (4, last_term)):
+        part = part + jnp.where(index == place, value, 0.0)
+
+    sums = all_totals(
+        n,
+        m,
+        4,
+        further.astype(BF),
+        tangent_row,
+        weight,
+        part,
+        start_norm,
+        hidden_gram,
+        tangent_gram,
+        gate_gram,
+        token_gram,
+        error_gram,
+    )
+    of_outer, of_change = sums[0, 0], sums[1, 0]
     change_up = contract_first(tangent_gate, gathered)
     change_down = contract_first(
         jnp.concatenate([tangent_hidden, hidden], axis=0), two_errors

time: 158 us -> 132 us (0.84)
  between operations: 16 us -> 0.92 us
  matrix products: 40.4 us -> 32.8 us
  other arithmetic: 9.09 us -> 3.38 us
  local copies, waits for them, and re-layouts: 2.57 us -> 4.57 us
    reduce_sum x2 -> x0, other arithmetic: 7.01 us -> none  [the longest x1 6.29 us: body(): jnp.sum(jnp.square(outer_up.astype(F32)))]
    dot_general x9, matrix products: 15.6 us -> 9.83 us  [contract_last(): lax.dot_general(left_side, right_side, (((1,), (1,)), ((), ())), preferre...]
    dot_general x5, matrix products: 12.7 us -> 10.3 us  [product(): return jnp.dot(left_side, right_side, preferred_element_type=F32)]
    unnamed x30 -> x19, local copies, waits for them, and re-layouts: 0.99 us -> 3.02 us
where the time goes in v2:
time: 132 us; the launch traced here: 131 us
  Pallas kernels  89.8 us (68%)
  matrix products  32.8 us (25%)
  local copies, waits for them, and re-layouts  4.57 us (3%)
  other arithmetic  3.38 us (3%)
    pallas_call x5, Pallas kernels, call(): pl.pallas_call(kernel, out_shape=outs, in_specs=[pl.BlockSpec(memory_spac...  89.8 us
    dot_general x2, matrix products, contract_first(): lax.dot_general(left_side, right_side, (((0,), (0,)), ((), ())), preferre...  12.6 us
    dot_general x5, matrix products, product(): return jnp.dot(left_side, right_side, preferred_element_type=F32)  10.3 us
    dot_general x9, matrix products, contract_last(): lax.dot_general(left_side, right_side, (((1,), (1,)), ((), ())), preferre...  9.83 us
    unnamed x19, local copies, waits for them, and re-layouts  3.02 us

profile of v2, /device:TPU:0, one launch (start us, length us, event | category | flops | bytes accessed | tf_op | source)
XLA Modules:
  0.0 131.5 jit_solution(10728690006687859911)
XLA Ops:
  0.6 0.7 convert_element_type.59
  1.3 0.1 broadcast_in_dim.28.refs_1_
  1.4 0.0 copy-start
  1.4 2.2 %copy-done = bf16[2368,896]{1,0:T(8,128)(2,1)S(1)} copy-done((bf16[2368,896]{1,0:T(8,128)(2,1)S(1)}, bf16[2368,896]{1,0:T(8,128)(2,1)}, u32[]{:S(2)}) %copy-start) | copy-done | bytes 4243480
  3.6 0.7 copy-done.2
  4.3 11.7 %shard_map.86 = (bf16[128,896]{1,0:T(8,128)(2,1)S(1)}, f32[128,128]{1,0:T(8,128)S(1)}, f32[8,128]{1,0:T(8,128)S(1)}) custom-call(bf16[2368,896]{1,0:T(8,128)(2,1)S(1)} %copy-done, bf16[2368,896]{1,0:T(8,128)(2,1)} %down_ref.1, bf16[16,896]{1,0:T(8,128)(2,1)S(1)} %copy-done.2, f32[16,128]{1,0:T(8,128)S(1)} %broadcast_in_dim.28.refs_1_), custom_call_target="tpu_custom_call" | custom-call | tf_op jit(solution)/shard_map/pallas_call | solution.py:64
  16.0 0.1 slice_reduce_fusion
  16.2 0.2 convert_reduce_fusion
  16.3 0.1 broadcast_in_dim.29.weight_ref
  16.4 0.2 fusion.39.refs_1_.token_ref
  16.7 1.3 convolution_convert_fusion
  18.0 0.3 copy.32.refs_1_
  18.3 3.5 %convolution_convert_fusion.1 = bf16[128,2368]{0,1:T(8,128)(2,1)S(1)} fusion(bf16[128,896]{1,0:T(8,128)(2,1)S(1)} %get-tuple-element.12, bf16[2368,896]{1,0:T(8,128)(2,1)} %param.10), kind=kOutput, calls=%fused_computation.3 | convolution fusion | flops 543465472 | bytes 5079040 | tf_op jit(solution)/shard_map/dot_general | solution.py:26
  21.7 0.3 copy.31.refs_0_
  22.1 19.4 %shard_map.87 = (bf16[128,2368]{1,0:T(8,128)(2,1)S(1)}, bf16[128,2368]{1,0:T(8,128)(2,1)S(1)}) custom-call(bf16[128,2368]{1,0:T(8,128)(2,1)S(1)} %copy.31.refs_0_, bf16[128,2368]{1,0:T(8,128)(2,1)S(1)} %copy.32.refs_1_), custom_call_target="tpu_custom_call" | custom-call | tf_op jit(solution)/shard_map/pallas_call | solution.py:64
  41.5 0.6 fusion.4
  42.1 0.0 slice-start.2
  42.1 0.3 fusion.40.tangent_ref
  42.5 0.0 slice-start.3
  42.5 0.0 slice-start.4
  42.5 3.9 %fusion = f32[256,896]{1,0:T(8,128)S(1)} fusion(bf16[2368,896]{1,0:T(8,128)(2,1)} %param.11, bf16[128,2368]{1,0:T(8,128)(2,1)S(1)} %get-tuple-element.29, bf16[128,2368]{1,0:T(8,128)(2,1)S(1)} %get-tuple-element.28), kind=kOutput, calls=%fused_computation.15 | convolution fusion | flops 1088749568 | bytes 6373376 | tf_op jit(solution)/shard_map/dot_general | solution.py:38
  46.4 0.0 slice-done.2
  46.4 0.0 slice-done.3
  46.4 0.0 copy-start.1
  46.5 0.0 slice-start.5
  46.5 1.0 fusion.24.z_ref
  47.5 0.0 copy-done.1
  47.5 26.7 %shard_map.88 = (bf16[128,896]{1,0:T(8,128)(2,1)S(1)}, bf16[128,896]{1,0:T(8,128)(2,1)S(1)}, f32[16,896]{1,0:T(8,128)S(1)}) custom-call(bf16[128,896]{1,0:T(8,128)(2,1)S(1)} %slice.61.y_ref, bf16[128,896]{1,0:T(8,128)(2,1)S(1)} %fusion.24.z_ref, bf16[16,896]{1,0:T(8,128)(2,1)S(1)} %copy-done.1, f32[16,128]{1,0:T(8,128)S(1)} %broadcast_in_dim.29.weight_ref), custom_call_target="tpu_custom_call" | custom-call | tf_op jit(solution)/shard_map/pallas_call | solution.py:64
  74.3 0.3 fusion.42.error_ref
  74.6 0.0 slice-done.4
  74.6 0.0 slice-done.5
  74.7 1.6 %fusion.38 = f32[256,2368]{1,0:T(8,128)S(1)} fusion(bf16[256,896]{1,0:T(8,128)(2,1)S(1)} %constant_dynamic-update-slice_fusion, bf16[2368,896]{1,0:T(8,128)(2,1)S(1)} %bitcast.31), kind=kOutput, calls=%fused_computation.69 | convolution fusion | flops 1086324736 | bytes 7127040 | tf_op jit(solution)/shard_map/dot_general | solution.py:26
  76.2 1.5 %fusion.17 = (bf16[128,2368]{1,0:T(8,128)(2,1)S(1)}, f32[128,2368]{1,0:T(8,128)S(1)}) fusion(f32[256,2368]{1,0:T(8,128)S(1)} %fusion.38, bf16[128,2368]{1,0:T(8,128)(2,1)S(1)} %get-tuple-element.14, bf16[128,2368]{1,0:T(8,128)(2,1)S(1)} %get-tuple-element.13, bf16[128,896]{1,0:T(8,128)(2,1)S(1)} %get-tuple-element.16, bf16[2368,896]{1,0:T(8,128)(2,1)S(1)} %bitcast.29), kind=kOutput, calls=%fused_computation.33 | convolution fusion | flops 549527552 | bytes 9928704 | tf_op jit(solution)/shard_map/dot_general | solution.py:26
  77.8 13.1 %shard_map.89 = (bf16[128,2368]{1,0:T(8,128)(2,1)S(1)}, f32[128,128]{1,0:T(8,128)S(1)}) custom-call(bf16[128,2368]{1,0:T(8,128)(2,1)S(1)} %get-tuple-element.32.refs_0_, f32[128,128]{1,0:T(8,128)S(1)} %fusion.39.refs_1_.token_ref), custom_call_target="tpu_custom_call" | custom-call | tf_op jit(solution)/shard_map/pallas_call | solution.py:64
  90.9 2.2 %fusion.6 = (f32[]{:T(128)}, f32[]{:T(128)}, f32[]{:T(128)}, bf16[128,2368]{1,0:T(8,128)(2,1)S(1)}) fusion(bf16[128,2368]{1,0:T(8,128)(2,1)S(1)} %get-tuple-element.14, f32[128,2368]{1,0:T(8,128)S(1)} %get-tuple-element.33, bf16[128,2368]{1,0:T(8,128)(2,1)S(1)} %get-tuple-element.28, f32[256,2368]{1,0:T(8,128)S(1)} %fusion.38, ...), kind=kOutput, calls=%fused_computation.21 | convolution fusion | flops 167747584 | bytes 5521420 | tf_op jit(solution)/shard_map/dot_general | solution.py:38
  93.1 1.9 %fusion.31 = f32[8]{0:T(128)S(1)} fusion(f32[]{:T(128)} %get-tuple-element.24, f32[]{:T(128)} %get-tuple-element.23, f32[]{:T(128)} %get-tuple-element.22), kind=kLoop, calls=%fused_computation.62 | loop fusion | flops 64 | bytes 44 | tf_op jit(solution)/shard_map/add | solution.py:449
  95.0 0.1 iota.13.part_ref
  95.1 0.3 fusion.41.gate_ref
  95.4 0.7 fusion.1.hidden_ref
  96.2 0.2 fusion.26
  96.4 0.0 slice-start
  96.4 3.1 %fusion.25.w_ref = bf16[128,896]{1,0:T(8,128)(2,1)S(1)} fusion(f32[128,896]{1,0:T(8,128)S(1)} %fusion.26, bf16[128,2368]{1,0:T(8,128)(2,1)S(1)} %get-tuple-element.25, bf16[2368,896]{1,0:T(8,128)(2,1)} %param.11), kind=kOutput, calls=%fused_computation.46 | convolution fusion | flops 543391744 | bytes 5537792 | tf_op jit(solution)/shard_map/dot_general | solution.py:38
  99.5 18.8 %shard_map.90 = f32[2,128]{1,0:T(2,128)S(1)} custom-call(bf16[128,896]{1,0:T(8,128)(2,1)S(1)} %fusion.25.w_ref, f32[16,896]{1,0:T(8,128)S(1)} %get-tuple-element.20.row_ref, f32[16,128]{1,0:T(8,128)S(1)} %broadcast_in_dim.29.weight_ref, f32[8,128]{1,0:T(8,128)S(1)} %iota.13.part_ref, f32[8,128]{1,0:T(8,128)S(1)} %get-tuple-element.21.norm_ref, ...), custom_call_target="tpu_custom_call" | custom-call | tf_op jit(solution)/shard_map/pallas_call | solution.py:64
  118.3 0.6 fusion.37
  118.9 6.6 %multiply_add_fusion = f32[2368,896]{1,0:T(8,128)} fusion(bf16[2368,896]{1,0:T(8,128)(2,1)S(1)} %bitcast.29, bf16[256,896]{1,0:T(8,128)(2,1)S(1)} %constant_dynamic-update-slice_fusion, f32[]{:T(128)} %bitcast.1, f32[]{:T(128)} %bitcast, bf16[128,2368]{1,0:T(8,128)(2,1)S(1)} %get-tuple-element.29, bf16[128,2368]{1,0:T(8,128)(2,1)S(1)} %get-tuple-element.28), kind=kOutput, calls=%fused_computation | convolution fusion | flops 1097236480 | bytes 14401544 | tf_op jit(solution)/shard_map/dot_general | solution.py:32
  125.5 0.0 slice-done
  125.5 0.0 slice-done.1
  125.5 6.0 %multiply_add_fusion.1 = f32[2368,896]{1,0:T(8,128)} fusion(bf16[2368,896]{1,0:T(8,128)(2,1)S(1)} %bitcast.27, bf16[128,2368]{1,0:T(8,128)(2,1)S(1)} %get-tuple-element.19, bf16[128,896]{1,0:T(8,128)(2,1)S(1)} %get-tuple-element.12, f32[]{:T(128)} %bitcast.1, f32[]{:T(128)} %bitcast), kind=kOutput, calls=%fused_computation.1 | convolution fusion | flops 551649280 | bytes 13565960 | tf_op jit(solution)/shard_map/dot_general | solution.py:32
  (10 shorter events, 0.1 us)
Async XLA Ops:
  1.4 2.2 %copy-start = (bf16[2368,896]{1,0:T(8,128)(2,1)S(1)}, bf16[2368,896]{1,0:T(8,128)(2,1)}, u32[]{:S(2)}) copy-start(bf16[2368,896]{1,0:T(8,128)(2,1)} %up_ref.1) | copy-start | bytes 12730372
  3.6 0.7 copy-start.2
  42.1 4.3 %slice-start.2 = ((s8[4243456]{0:T(1024)(128)(4,1)}), s8[4194304]{0:T(1024)(128)(4,1)S(1)}, s32[]{:S(2)}) async-start(s8[4243456]{0:T(1024)(128)(4,1)} %bitcast.28), calls=%async_computation.2 | async-start | bytes 8388608
  42.5 3.9 %slice-start.3 = ((s8[4243456]{0:T(1024)(128)(4,1)}), s8[49152]{0:T(1024)(128)(4,1)S(1)}, s32[]{:S(2)}) async-start(s8[4243456]{0:T(1024)(128)(4,1)} %bitcast.28), calls=%async_computation.3 | async-start | bytes 98304
  42.5 32.1 %slice-start.4 = ((s8[4243456]{0:T(1024)(128)(4,1)}), s8[4194304]{0:T(1024)(128)(4,1)S(1)}, s32[]{:S(2)}) async-start(s8[4243456]{0:T(1024)(128)(4,1)} %bitcast.30), calls=%async_computation.4 | async-start | bytes 8388608
  46.4 1.0 copy-start.1
  46.5 28.2 %slice-start.5 = ((s8[4243456]{0:T(1024)(128)(4,1)}), s8[49152]{0:T(1024)(128)(4,1)S(1)}, s32[]{:S(2)}) async-start(s8[4243456]{0:T(1024)(128)(4,1)} %bitcast.30), calls=%async_computation.5 | async-start | bytes 98304
  96.4 29.0 %slice-start = ((s8[4243456]{0:T(1024)(128)(4,1)}), s8[49152]{0:T(1024)(128)(4,1)S(1)}, s32[]{:S(2)}) async-start(s8[4243456]{0:T(1024)(128)(4,1)} %bitcast.26), calls=%async_computation | async-start | bytes 98304
  118.9 6.6 %slice-start.1 = ((s8[4243456]{0:T(1024)(128)(4,1)}), s8[4194304]{0:T(1024)(128)(4,1)S(1)}, s32[]{:S(2)}) async-start(s8[4243456]{0:T(1024)(128)(4,1)} %bitcast.26), calls=%async_computation.1 | async-start | bytes 8388608
